TPU v7x, 32 devices: a whole 2x2x4 slice. The times are simulated.
32 devices in a mesh: slab: 8 (over z, core), sub: 4 (over y, x).
Axes of the slice: x: 2, y: 2, z: 4, core: 2. Of those that a mesh axis runs over, the one named last changes fastest.
Arguments:
- child_moments: bfloat16 [216, 32768], P(None, ('slab', 'sub')), may hold values from -6 to 6
- incoming: bfloat16 [216, 4096], P(None, ('slab', 'sub')), may hold values from -6 to 6
- m2m_ops: bfloat16 [8, 216, 216], replicated, may hold values from -0.15625 to 0.15625
- m2l_ops: bfloat16 [160, 216, 216], P('sub'), may hold values from -0.046875 to 0.046875
- l2l_ops: bfloat16 [8, 216, 216], replicated, may hold values from -0.4375 to 0.4375
- partners: int32 [160, 4096], P(None, ('slab', 'sub')), may hold values from -1 to 4095, as said below
Outputs:
- child_locals: float32 [216, 32768], P(None, ('slab', 'sub'))
Inputs may be any that keep to these rules, and one draw needn't show every extreme that they name: `partners`: cells are numbered in Morton order of bricks of the domain, each brick one cell wide along the first dimension; the source of a pair lies in the same slab as its target or in an adjacent one, that is its id divided by 128 * 4 differs from the target's by at most one. Pairs are those of the interaction list: source and target are not adjacent, their parents are.
All inputs are finite; a program needn't handle non-finite values.
Results may differ from a plain program's by a relative error of at most 0.0035.
Values may be sent and summed in bfloat16 or wider, within the bound.
No kernel may reach another device: no remote copies, remote signals or barrier semaphores. Data moves between devices by JAX's collectives and lax.ppermute only.
A program may use at most 128 MiB of HBM per device.

v0:
```python
import functools

import jax
import jax.numpy as jnp
from jax import lax
from jax.experimental import pallas as pl
from jax.experimental.pallas import tpu as pltpu
from jax.sharding import PartitionSpec as P


RIM = 32
TILE = 256
LANES = 128
GROUP = 8
VMEM = pl.BlockSpec(memory_space=pltpu.VMEM)
ANY = pl.BlockSpec(memory_space=pl.ANY)
HBM = pl.BlockSpec(memory_space=pltpu.HBM)
BF16 = jnp.bfloat16
F32 = jnp.float32


def swap(x, r, n):
    if r == 0:
        return x
    return lax.ppermute(x, "sub", [(i, i ^ r) for i in range(n)])


def one_hot(mask):
    return jnp.where(mask, jnp.ones((), BF16), jnp.zeros((), BF16))


def by_group(groups, parts, shift):
    out = parts[shift % 4]
    for g in range(1, 4):
        out = jnp.where(groups == jnp.full((), g, groups.dtype), parts[(g + shift) % 4], out)
    return out


def iota(shape, dim):
    return lax.broadcasted_iota(jnp.int32, shape, dim)


def up_kernel(n_sub, cells, child_hbm, ops_hbm, partners_hbm, *refs):
    outs, refs = refs[:n_sub], refs[n_sub:]
    to_pair, to_other, child, ops, partners, sems = refs
    copies = [
        pltpu.make_async_copy(src, dst, sems.at[i])
        for i, (src, dst) in enumerate([(partners_hbm, partners), (child_hbm, child), (ops_hbm, ops)])
    ]
    for copy in copies:
        copy.start()
    order = child.shape[0]
    lane = iota((1, TILE), 1)
    row = iota((TILE, TILE), 0).astype(F32).astype(BF16)

    copies[0].wait()
    n_ops = partners.shape[0] // n_sub
    my_slab = lax.axis_index("slab")
    me = lax.axis_index("sub")
    for r in range(n_sub):
        q = me ^ r
        ids = partners[pl.ds(pl.multiple_of(q * n_ops, n_ops), n_ops), :]
        safe = jnp.maximum(ids, 0)
        source = lax.div(safe, cells)
        inner = safe - source * cells
        slab = lax.div(source, n_sub)
        block = (source - slab * n_sub) ^ q
        delta = slab - my_slab
        rim_at = n_sub * cells + block * (2 * RIM)
        column = jnp.where(
            delta == 0,
            block * cells + inner,
            jnp.where(delta < 0, rim_at + inner - (cells - RIM), rim_at + RIM + inner),
        )
        code = lax.shift_left(LANES + (column & (LANES - 1)), lax.shift_right_logical(column, 7))
        outs[r][order:, :] = jnp.where(ids >= 0, code, 0).astype(F32).astype(BF16)

    copies[1].wait()
    group = lax.shift_right_logical(lane, 5)
    chunks = []
    for q in range(4):
        want = 8 * (lane & (RIM - 1)) + 4 * lax.shift_right_logical(lane, 7) + ((group - q) & 3)
        hot = one_hot(row == jnp.broadcast_to(want.astype(F32).astype(BF16), (TILE, TILE)))
        chunk = jnp.dot(child[:, q * TILE : (q + 1) * TILE], hot, preferred_element_type=F32)
        chunks.append(chunk.astype(BF16))
    groups = jnp.broadcast_to(group[:, :LANES].astype(F32).astype(BF16), (order, LANES))
    copies[2].wait()
    total = None
    for j in range(4):
        turned = None
        for o in (j, j + 4):
            half = [x[:, o // 4 * LANES : (o // 4 + 1) * LANES] for x in chunks]
            part = jnp.dot(ops[o], by_group(groups, half, -j), preferred_element_type=F32)
            turned = part if turned is None else turned + part
        turned = turned if j == 0 else pltpu.roll(turned, LANES - RIM * j, 1)
        total = turned if total is None else total + turned
    total = total.astype(BF16)
    for r in range(n_sub):
        outs[r][:order, :] = total
    low, high = total[:, :RIM], total[:, cells - RIM :]
    even = lax.rem(my_slab, 2) == 0
    to_pair[...] = jnp.where(even, high, low)
    to_other[...] = jnp.where(even, low, high)


def up(child, ops, partners, n_sub):
    order = child.shape[0]
    cells = child.shape[1] // 8
    n_ops = partners.shape[0] // n_sub
    return pl.pallas_call(
        functools.partial(up_kernel, n_sub, cells),
        out_shape=[jax.ShapeDtypeStruct((order + n_ops, cells), BF16)] * n_sub
        + [jax.ShapeDtypeStruct((order, RIM), BF16)] * 2,
        in_specs=[HBM] * 3,
        out_specs=[VMEM] * (n_sub + 2),
        scratch_shapes=[
            pltpu.VMEM(child.shape, BF16),
            pltpu.VMEM(ops.shape, BF16),
            pltpu.VMEM(partners.shape, jnp.int32),
            pltpu.SemaphoreType.DMA((3,)),
        ],
        compiler_params=pltpu.CompilerParams(vmem_limit_bytes=16 << 20),
        cost_estimate=pl.CostEstimate(flops=1 << 30, bytes_accessed=2 << 20, transcendentals=0),
        name="up",
    )(*[pltpu.with_memory_space_constraint(x, pltpu.HBM) for x in (child, ops, partners)])


def spans_of(n_ops):
    return [(w, min(w + 32, n_ops)) for w in range(0, n_ops, 32)]


def pack(hit, n_ops):
    word = jnp.where(hit > 0.0, lax.shift_left(1, iota((n_ops, 1), 0) & 31), 0)
    return [jnp.sum(word[w:end]) for w, end in spans_of(n_ops)]


def each_bit(words, act, state):
    for i, word in enumerate(words):

        def step(carry, i=i):
            word, state = carry
            return word & (word - 1), act(32 * i + 31 - lax.clz(word & -word), state)

        state = lax.while_loop(lambda carry: carry[0] != 0, step, (word, state))[1]
    return state


def list_units(order, loads, n_ops, idx, code0, todo):
    cells = loads[0].shape[1]
    n_tiles = idx.shape[0]
    per = TILE // cells
    rows = iota((TILE, LANES), 0)
    code0[...] = lax.shift_left(LANES + (rows & (LANES - 1)), lax.shift_right_logical(rows, 7)).astype(F32).astype(BF16)
    hits = []
    for n in range(n_tiles):
        table = jnp.concatenate([x[order:, :].astype(F32) for x in loads[n * per : (n + 1) * per]], axis=1)
        idx[n, 0:n_ops, :] = table
        idx[n, n_ops : n_ops + 8, :] = jnp.zeros((8, TILE), F32)
        hits.append(jnp.max(table, axis=1, keepdims=True))
    count = jnp.int32(0)
    for n in range(n_tiles):

        def add(k, count, n=n):
            todo[count] = k * n_tiles + n
            return count + 1

        count = each_bit(pack(hits[n], n_ops), add, count)
    for a in range(GROUP):
        todo[count + a] = n_ops * n_tiles
    return hits, count, lax.div(count + GROUP - 1, GROUP)


def one_hots(row, base, first_tile, n_tiles):
    for t in range(first_tile, first_tile + n_tiles):
        scaled = (row * (4.0**-t)).astype(BF16)
        yield jnp.concatenate(
            [
                one_hot(base == jnp.broadcast_to(scaled[:, c : c + LANES], (TILE, LANES)))
                for c in range(0, TILE, LANES)
            ],
            axis=1,
        )


def pick_kernel(order, n_sub, *refs):
    loads, refs = refs[:n_sub], refs[n_sub:]
    ops_hbm, picked, ops, win, idx, code0, todo, sems = refs
    n_ops = ops.shape[0]
    n_tiles, k_tiles = idx.shape[0], win.shape[0]
    cells = loads[0].shape[1]
    for r in range(n_sub):
        win[r * cells // TILE, :, r * cells % TILE : r * cells % TILE + cells] = loads[r][:order, :]
    hits, _, trips = list_units(order, loads, n_ops, idx, code0, todo)

    used = jnp.where(iota((n_ops, 1), 0) == n_ops - 1, 1.0, functools.reduce(jnp.maximum, hits))
    used = pack(used, n_ops)

    def copy_in(k):
        return pltpu.make_async_copy(ops_hbm.at[k], ops.at[k], sems.at[k])

    def start(k, state):
        copy_in(k).start()
        return state

    def wait(k, state):
        copy_in(k).wait()
        return state

    each_bit(used, start, jnp.int32(0))

    def body(i, carry):
        base = code0[...]
        for a in range(GROUP):
            u = todo[GROUP * i + a]
            k = lax.div(u, n_tiles)
            row = idx[u - k * n_tiles, pl.ds(k, 1), :]
            total = None
            for t, hot in enumerate(one_hots(row, base, 0, k_tiles)):
                part = jnp.dot(win[t], hot, preferred_element_type=F32)
                total = part if total is None else total + part
            picked[GROUP * i + a] = total.astype(BF16)
        return carry

    lax.fori_loop(0, trips, body, 0)
    each_bit(used, wait, jnp.int32(0))


def apply_kernel(order, n_sub, *refs):
    loads, sides, refs = refs[:n_sub], refs[n_sub : 2 * n_sub], refs[2 * n_sub :]
    picked, ops, refs = refs[0], refs[1], refs[2:]
    outs, (win, idx, code0, acc, cols, todo) = refs[:n_sub], refs[n_sub:]
    n_ops = ops.shape[0]
    n_tiles, k_tiles = idx.shape[0], win.shape[0]
    cells = loads[0].shape[1]
    for i in range(0, n_sub, 2):
        at = i // 2 * LANES
        pair = jnp.concatenate([sides[i][...], sides[i + 1][...]], axis=1)
        win[at // TILE, :, at % TILE : at % TILE + LANES] = pair
    _, _, trips = list_units(order, loads, n_ops, idx, code0, todo)
    acc[...] = jnp.zeros_like(acc)

    def gather(i):
        base = code0[...]
        for a in range(GROUP):
            u = todo[GROUP * i + a]
            k = lax.div(u, n_tiles)
            row = idx[u - k * n_tiles, pl.ds(k, 1), :]
            total = None
            for t, hot in enumerate(one_hots(row, base, n_sub * cells // TILE, k_tiles)):
                part = jnp.dot(win[t], hot, preferred_element_type=F32)
                total = part if total is None else total + part
            cols[i & 1, a] = total.astype(BF16) + picked[GROUP * i + a]

    def apply(i):
        for a in range(GROUP):
            u = todo[GROUP * i + a]
            k = lax.div(u, n_tiles)
            acc[u - k * n_tiles] += jnp.dot(
                ops[jnp.minimum(k, n_ops - 1)], cols[i & 1, a], preferred_element_type=F32
            )

    def body(i, carry):
        apply(i - 1)
        gather(i)
        return carry

    @pl.when(trips > 0)
    def _():
        gather(0)
        lax.fori_loop(1, trips, body, 0)
        apply(trips - 1)

    for j, out in enumerate(outs):
        out[...] = acc[j * cells // TILE, :, j * cells % TILE : j * cells % TILE + cells].astype(out.dtype)


def m2l_sizes(loads, ops):
    n_sub, cells = len(loads), loads[0].shape[1]
    n_tiles = n_sub * cells // TILE
    return n_sub, cells, n_tiles, ops.shape[0] * n_tiles + GROUP


def pick(loads, ops, order):
    n_sub, cells, n_tiles, units = m2l_sizes(loads, ops)
    n_ops = ops.shape[0]
    return pl.pallas_call(
        functools.partial(pick_kernel, order, n_sub),
        out_shape=[jax.ShapeDtypeStruct((units, order, TILE), BF16), jax.ShapeDtypeStruct(ops.shape, BF16)],
        in_specs=[VMEM] * n_sub + [HBM],
        out_specs=[VMEM] * 2,
        scratch_shapes=[
            pltpu.VMEM((n_sub * cells // TILE, order, TILE), BF16),
            pltpu.VMEM((n_tiles, n_ops + 8, TILE), F32),
            pltpu.VMEM((TILE, LANES), BF16),
            pltpu.SMEM((units,), jnp.int32),
            pltpu.SemaphoreType.DMA((n_ops,)),
        ],
        compiler_params=pltpu.CompilerParams(vmem_limit_bytes=24 << 20),
        cost_estimate=pl.CostEstimate(flops=4 << 30, bytes_accessed=4 << 20, transcendentals=0),
        name="pick",
    )(*loads, pltpu.with_memory_space_constraint(ops, pltpu.HBM))


def apply_ops(loads, sides, picked, ops, order):
    n_sub, cells, n_tiles, units = m2l_sizes(loads, ops)
    n_ops = ops.shape[0]
    return pl.pallas_call(
        functools.partial(apply_kernel, order, n_sub),
        out_shape=[jax.ShapeDtypeStruct((order, cells), F32 if r == 0 else BF16) for r in range(n_sub)],
        in_specs=[VMEM] * (2 * n_sub + 2),
        out_specs=[VMEM] * n_sub,
        scratch_shapes=[
            pltpu.VMEM((n_sub * 2 * RIM // TILE, order, TILE), BF16),
            pltpu.VMEM((n_tiles, n_ops + 8, TILE), F32),
            pltpu.VMEM((TILE, LANES), BF16),
            pltpu.VMEM((n_tiles, order, TILE), F32),
            pltpu.VMEM((2, GROUP, order, TILE), BF16),
            pltpu.SMEM((units,), jnp.int32),
        ],
        compiler_params=pltpu.CompilerParams(vmem_limit_bytes=24 << 20),
        cost_estimate=pl.CostEstimate(flops=4 << 30, bytes_accessed=4 << 20, transcendentals=0),
        name="apply",
    )(*loads, *sides, picked, ops)


def down_kernel(n_parts, incoming, *refs):
    parts = refs[:n_parts]
    ops, out, stage, sem = refs[n_parts:]
    cells = incoming.shape[1]
    far = parts[0][...].astype(F32)
    for r in range(1, n_parts):
        far = far + parts[r][...].astype(F32)
    held = (incoming[...].astype(F32) + far).astype(BF16)
    order = held.shape[0]
    lane = iota((1, TILE), 1)
    row = iota((TILE, LANES), 0)
    base = 8 * (row & (RIM - 1)) + 4 * lax.shift_right_logical(row, 7)
    quarter = lax.shift_right_logical(row, 5)
    lane16 = lane.astype(F32).astype(BF16)
    groups = jnp.broadcast_to(lax.shift_right_logical(lane[:, :LANES], 5), (order, LANES))
    wide = held.astype(F32)
    turned = [held] + [pltpu.roll(wide, RIM * j, 1).astype(BF16) for j in range(1, 4)]
    made = [jnp.dot(ops[o], turned[o % 4], preferred_element_type=F32) for o in range(8)]
    copies = []
    for q in range(8 * cells // TILE):
        have = (base + ((quarter - q) & 3)).astype(F32).astype(BF16)
        hot = jnp.concatenate(
            [one_hot(have == jnp.broadcast_to(lane16[:, c : c + LANES], (TILE, LANES))) for c in (0, LANES)], axis=1
        )
        rest = jnp.concatenate([by_group(groups, made[4 * h : 4 * h + 4], -q) for h in range(2)], axis=1)
        total = None
        for _ in range(2):
            top = rest.astype(BF16)
            part = jnp.dot(top, hot, preferred_element_type=F32)
            total = part if total is None else total + part
            rest = rest - top.astype(F32)
        stage[q] = total
        copy = pltpu.make_async_copy(stage.at[q], out.at[:, q * TILE : (q + 1) * TILE], sem.at[q])
        copy.start()
        copies.append(copy)
    for copy in copies:
        copy.wait()


def down(incoming, parts, ops):
    order, cells = incoming.shape
    chunks = 8 * cells // TILE
    return pl.pallas_call(
        functools.partial(down_kernel, len(parts)),
        out_shape=jax.ShapeDtypeStruct((order, 8 * cells), F32),
        in_specs=[VMEM] * (len(parts) + 2),
        out_specs=pl.BlockSpec(memory_space=pl.ANY),
        scratch_shapes=[pltpu.VMEM((chunks, order, TILE), F32), pltpu.SemaphoreType.DMA((chunks,))],
        compiler_params=pltpu.CompilerParams(vmem_limit_bytes=16 << 20),
        cost_estimate=pl.CostEstimate(flops=1 << 30, bytes_accessed=2 << 20, transcendentals=0),
        name="down",
    )(incoming, *parts, ops)


def far_field(child_moments, incoming, m2m_ops, m2l_ops, l2l_ops, partners):
    order, cells = incoming.shape
    n_sub = lax.axis_size("sub")
    n_slab = lax.axis_size("slab")
    assert n_sub & (n_sub - 1) == 0 and n_slab % 2 == 0 and cells == LANES == 4 * RIM
    *sends, to_pair, to_other = up(child_moments, m2m_ops, partners, n_sub)
    got_pair = lax.ppermute(to_pair, "slab", [(i, i ^ 1) for i in range(n_slab)])
    got_other = lax.ppermute(to_other, "slab", [(i, ((i + 1) ^ 1) - 1) for i in range(1, n_slab - 1)])
    loads = [swap(sends[r], r, n_sub) for r in range(n_sub)]
    even = lax.axis_index("slab") % 2 == 0
    rim = jnp.concatenate(
        [jnp.where(even, got_other, got_pair), jnp.where(even, got_pair, got_other)], axis=1
    )
    sides = [swap(rim, r, n_sub) for r in range(n_sub)]
    picked, held_ops = pick(loads, m2l_ops, order)
    mine, *others = apply_ops(loads, sides, picked, held_ops, order)
    back = [swap(x, r + 1, n_sub) for r, x in reversed(list(enumerate(others)))]
    return down(incoming, [mine, *back], l2l_ops)


def solution(mesh):
    in_specs = (
        P(None, ("slab", "sub")),
        P(None, ("slab", "sub")),
        P(),
        P("sub", None, None),
        P(),
        P(None, ("slab", "sub")),
    )
    out_specs = P(None, ("slab", "sub"))
    return jax.shard_map(far_field, mesh=mesh, in_specs=in_specs, out_specs=out_specs, check_vma=False)
```

profile of v0, /device:TPU:0, one launch (start us, length us, event | category | flops | bytes accessed | tf_op | source)
XLA Modules:
  0.0 28.9 jit_solution(4038967803553035109)
XLA Ops:
  0.0 2.1 %up.1 = (bf16[256,128]{1,0:T(8,128)(2,1)S(1)}, bf16[256,128]{1,0:T(8,128)(2,1)S(1)}, bf16[256,128]{1,0:T(8,128)(2,1)S(1)}, bf16[256,128]{1,0:T(8,128)(2,1)S(1)},...) custom-call(bf16[216,1024]{1,0:T(8,128)(2,1)} %child_hbm.1, bf16[8,216,216]{2,1,0:T(8,128)(2,1)} %ops_hbm.1, ...), custom_call_target="tpu_custom_call" | custom-call | flops 1073741824 | bytes 2097152 | tf_op jit(solution)/shard_map/up/pallas_call | solution.py:110
  2.1 0.7 %collective-permute-start.3 = (bf16[216,32]{1,0:T(8,128)(2,1)S(1)}, bf16[216,32]{1,0:T(8,128)(2,1)S(1)}, u32[]{:S(2)}, u32[]{:S(2)}) collective-permute-start(bf16[216,32]{1,0:T(8,128)(2,1)S(1)} %get-tuple-element.21), channel_id=1, source_target_pairs={{4,8},{8,4},{12,16},{16,12},{20,24},{24,20},{5,9},{9,5},{13,17},{1... | collective-permute-start | bytes 41480 | tf_op jit(solution)/shard_map/ppermute | solution.py:387
  2.8 4.5 %collective-permute-start.4 = (bf16[216,32]{1,0:T(8,128)(2,1)S(1)}, bf16[216,32]{1,0:T(8,128)(2,1)S(1)}, u32[]{:S(2)}, u32[]{:S(2)}) collective-permute-start(bf16[216,32]{1,0:T(8,128)(2,1)S(1)} %get-tuple-element.22), channel_id=1, source_target_pairs={{0,4},{4,0},{8,12},{12,8},{16,20},{20,16},{24,28},{28,24},{1,5},{5... | collective-permute-start | bytes 41480 | tf_op jit(solution)/shard_map/ppermute | solution.py:386
  7.2 1.5 %collective-permute-start = (bf16[256,128]{1,0:T(8,128)(2,1)S(1)}, bf16[256,128]{1,0:T(8,128)(2,1)S(1)}, u32[]{:S(2)}, u32[]{:S(2)}) collective-permute-start(bf16[256,128]{1,0:T(8,128)(2,1)S(1)} %get-tuple-element.18), channel_id=1, source_target_pairs={{0,1},{1,0},{2,3},{3,2},{4,5},{5,4},{6,7},{7,6},{8,9},{9,8},{10,11... | collective-permute-start | bytes 196616 | tf_op jit(solution)/shard_map/ppermute | solution.py:25
  8.7 1.5 %collective-permute-start.1 = (bf16[256,128]{1,0:T(8,128)(2,1)S(1)}, bf16[256,128]{1,0:T(8,128)(2,1)S(1)}, u32[]{:S(2)}, u32[]{:S(2)}) collective-permute-start(bf16[256,128]{1,0:T(8,128)(2,1)S(1)} %get-tuple-element.19), channel_id=1, source_target_pairs={{0,2},{1,3},{2,0},{3,1},{4,6},{5,7},{6,4},{7,5},{8,10},{9,11},{10,... | collective-permute-start | bytes 196616 | tf_op jit(solution)/shard_map/ppermute | solution.py:25
  10.3 0.5 %collective-permute-start.2 = (bf16[256,128]{1,0:T(8,128)(2,1)S(1)}, bf16[256,128]{1,0:T(8,128)(2,1)S(1)}, u32[]{:S(2)}, u32[]{:S(2)}) collective-permute-start(bf16[256,128]{1,0:T(8,128)(2,1)S(1)} %get-tuple-element.20), channel_id=1, source_target_pairs={{0,3},{1,2},{2,1},{3,0},{4,7},{5,6},{6,5},{7,4},{8,11},{9,10},{10,... | collective-permute-start | bytes 196616 | tf_op jit(solution)/shard_map/ppermute | solution.py:25
  10.7 0.0 collective-permute-done.3
  10.7 0.0 collective-permute-done.4
  10.8 0.1 pad_maximum_fusion.refs_4_
  10.9 2.5 %collective-permute-start.7 = (bf16[216,64]{1,0:T(8,128)(2,1)S(1)}, bf16[216,64]{1,0:T(8,128)(2,1)S(1)}, u32[]{:S(2)}, u32[]{:S(2)}) collective-permute-start(bf16[216,64]{1,0:T(8,128)(2,1)S(1)} %pad_maximum_fusion.refs_4_), channel_id=1, source_target_pairs={{0,3},{1,2},{2,1},{3,0},{4,7},{5,6},{6,5},{7,4},{8,11},{9,10},{10,... | collective-permute-start | bytes 82952 | tf_op jit(solution)/shard_map/ppermute | solution.py:25
  13.4 0.5 %collective-permute-start.6 = (bf16[216,64]{1,0:T(8,128)(2,1)S(1)}, bf16[216,64]{1,0:T(8,128)(2,1)S(1)}, u32[]{:S(2)}, u32[]{:S(2)}) collective-permute-start(bf16[216,64]{1,0:T(8,128)(2,1)S(1)} %pad_maximum_fusion.refs_4_), channel_id=1, source_target_pairs={{0,2},{1,3},{2,0},{3,1},{4,6},{5,7},{6,4},{7,5},{8,10},{9,11},{10,... | collective-permute-start | bytes 82952 | tf_op jit(solution)/shard_map/ppermute | solution.py:25
  13.9 0.0 collective-permute-done.refs_1_
  13.9 0.5 %collective-permute-start.5 = (bf16[216,64]{1,0:T(8,128)(2,1)S(1)}, bf16[216,64]{1,0:T(8,128)(2,1)S(1)}, u32[]{:S(2)}, u32[]{:S(2)}) collective-permute-start(bf16[216,64]{1,0:T(8,128)(2,1)S(1)} %pad_maximum_fusion.refs_4_), channel_id=1, source_target_pairs={{0,1},{1,0},{2,3},{3,2},{4,5},{5,4},{6,7},{7,6},{8,9},{9,8},{10,11... | collective-permute-start | bytes 82952 | tf_op jit(solution)/shard_map/ppermute | solution.py:25
  14.4 0.0 collective-permute-done.1.refs_2_
  14.4 1.0 %collective-permute-done.2.refs_3_ = bf16[256,128]{1,0:T(8,128)(2,1)S(1)} collective-permute-done((bf16[256,128]{1,0:T(8,128)(2,1)S(1)}, bf16[256,128]{1,0:T(8,128)(2,1)S(1)}, u32[]{:S(2)}, u32[]{:S(2)}) %collective-permute-start.2) | collective-permute-done | bytes 65568 | tf_op jit(solution)/shard_map/ppermute | solution.py:25
  15.5 3.0 %pick.1 = (bf16[88,216,256]{2,1,0:T(8,128)(2,1)S(1)}, bf16[40,216,216]{2,1,0:T(8,128)(2,1)S(1)}) custom-call(bf16[256,128]{1,0:T(8,128)(2,1)S(1)} %get-tuple-element.17.refs_0_, bf16[256,128]{1,0:T(8,128)(2,1)S(1)} %collective-permute-done.refs_1_, bf16[256,128]{1,0:T(8,128)(2,1)S(1)} %collective-permute-done.1.refs_2_, ...), custom_call_target="tpu_custom_call" | custom-call | flops 4294967296 | bytes 4194304 | tf_op jit(solution)/shard_map/pick/pallas_call | solution.py:286
  18.5 0.0 collective-permute-done.7.refs_7_
  18.5 0.0 collective-permute-done.6.refs_6_
  18.5 0.0 collective-permute-done.5.refs_5_
  18.5 0.0 copy-start
  18.5 0.0 copy-start.1
  18.5 2.9 %apply.1 = (f32[216,128]{1,0:T(8,128)S(1)}, bf16[216,128]{1,0:T(8,128)(2,1)S(1)}, bf16[216,128]{1,0:T(8,128)(2,1)S(1)}, bf16[216,128]{1,0:T(8,128)(2,1)S(1)}) custom-call(bf16[256,128]{1,0:T(8,128)(2,1)S(1)} %get-tuple-element.17.refs_0_, bf16[256,128]{1,0:T(8,128)(2,1)S(1)} %collective-permute-done.refs_1_, ...), custom_call_target="tpu_custom_call" | custom-call | flops 4294967296 | bytes 4194304 | tf_op jit(solution)/shard_map/apply/pallas_call | solution.py:307
  21.5 1.5 %collective-permute-start.8 = (bf16[216,128]{1,0:T(8,128)(2,1)S(1)}, bf16[216,128]{1,0:T(8,128)(2,1)S(1)}, u32[]{:S(2)}, u32[]{:S(2)}) collective-permute-start(bf16[216,128]{1,0:T(8,128)(2,1)S(1)} %get-tuple-element.26), channel_id=1, source_target_pairs={{0,3},{1,2},{2,1},{3,0},{4,7},{5,6},{6,5},{7,4},{8,11},{9,10},{10,... | collective-permute-start | bytes 165896 | tf_op jit(solution)/shard_map/ppermute | solution.py:25
  23.0 0.0 collective-permute-start.9
  23.0 2.0 %collective-permute-start.10 = (bf16[216,128]{1,0:T(8,128)(2,1)S(1)}, bf16[216,128]{1,0:T(8,128)(2,1)S(1)}, u32[]{:S(2)}, u32[]{:S(2)}) collective-permute-start(bf16[216,128]{1,0:T(8,128)(2,1)S(1)} %get-tuple-element.28), channel_id=1, source_target_pairs={{0,1},{1,0},{2,3},{3,2},{4,5},{5,4},{6,7},{7,6},{8,9},{9,8},{10,11... | collective-permute-start | bytes 165896 | tf_op jit(solution)/shard_map/ppermute | solution.py:25
  25.0 1.6 %collective-permute-done.8.refs_1_ = bf16[216,128]{1,0:T(8,128)(2,1)S(1)} collective-permute-done((bf16[216,128]{1,0:T(8,128)(2,1)S(1)}, bf16[216,128]{1,0:T(8,128)(2,1)S(1)}, u32[]{:S(2)}, u32[]{:S(2)}) %collective-permute-start.8) | collective-permute-done | bytes 55328 | tf_op jit(solution)/shard_map/ppermute | solution.py:25
  26.6 0.6 %collective-permute-done.9.refs_2_ = bf16[216,128]{1,0:T(8,128)(2,1)S(1)} collective-permute-done((bf16[216,128]{1,0:T(8,128)(2,1)S(1)}, bf16[216,128]{1,0:T(8,128)(2,1)S(1)}, u32[]{:S(2)}, u32[]{:S(2)}) %collective-permute-start.9) | collective-permute-done | bytes 55328 | tf_op jit(solution)/shard_map/ppermute | solution.py:25
  27.2 0.0 collective-permute-done.10.refs_3_
  27.2 0.0 copy-done
  27.2 0.0 copy-done.1
  27.2 1.7 %down.1 = f32[216,1024]{1,0:T(8,128)} custom-call(bf16[216,128]{1,0:T(8,128)(2,1)S(1)} %copy-done.1, f32[216,128]{1,0:T(8,128)S(1)} %get-tuple-element.25.refs_0_, bf16[216,128]{1,0:T(8,128)(2,1)S(1)} %collective-permute-done.8.refs_1_, bf16[216,128]{1,0:T(8,128)(2,1)S(1)} %collective-permute-done.9.refs_2_, ...), custom_call_target="tpu_custom_call" | custom-call | flops 1073741824 | bytes 2097152 | tf_op jit(solution)/shard_map/down/pallas_call | solution.py:368
  (1 shorter events, 0.0 us)
Async XLA Ops:
  2.1 8.6 %collective-permute-start.3 = (bf16[216,32]{1,0:T(8,128)(2,1)S(1)}, bf16[216,32]{1,0:T(8,128)(2,1)S(1)}, u32[]{:S(2)}, u32[]{:S(2)}) collective-permute-start(bf16[216,32]{1,0:T(8,128)(2,1)S(1)} %get-tuple-element.21), channel_id=1, source_target_pairs={{4,8},{8,4},{12,16},{16,12},{20,24},{24,20},{5,9},{9,5},{13,17},{1... | collective-permute-start | bytes 41480 | tf_op jit(solution)/shard_map/ppermute | solution.py:387
  2.8 8.0 %collective-permute-start.4 = (bf16[216,32]{1,0:T(8,128)(2,1)S(1)}, bf16[216,32]{1,0:T(8,128)(2,1)S(1)}, u32[]{:S(2)}, u32[]{:S(2)}) collective-permute-start(bf16[216,32]{1,0:T(8,128)(2,1)S(1)} %get-tuple-element.22), channel_id=1, source_target_pairs={{0,4},{4,0},{8,12},{12,8},{16,20},{20,16},{24,28},{28,24},{1,5},{5... | collective-permute-start | bytes 41480 | tf_op jit(solution)/shard_map/ppermute | solution.py:386
  7.2 6.6 %collective-permute-start = (bf16[256,128]{1,0:T(8,128)(2,1)S(1)}, bf16[256,128]{1,0:T(8,128)(2,1)S(1)}, u32[]{:S(2)}, u32[]{:S(2)}) collective-permute-start(bf16[256,128]{1,0:T(8,128)(2,1)S(1)} %get-tuple-element.18), channel_id=1, source_target_pairs={{0,1},{1,0},{2,3},{3,2},{4,5},{5,4},{6,7},{7,6},{8,9},{9,8},{10,11... | collective-permute-start | bytes 196616 | tf_op jit(solution)/shard_map/ppermute | solution.py:25
  8.7 5.7 %collective-permute-start.1 = (bf16[256,128]{1,0:T(8,128)(2,1)S(1)}, bf16[256,128]{1,0:T(8,128)(2,1)S(1)}, u32[]{:S(2)}, u32[]{:S(2)}) collective-permute-start(bf16[256,128]{1,0:T(8,128)(2,1)S(1)} %get-tuple-element.19), channel_id=1, source_target_pairs={{0,2},{1,3},{2,0},{3,1},{4,6},{5,7},{6,4},{7,5},{8,10},{9,11},{10,... | collective-permute-start | bytes 196616 | tf_op jit(solution)/shard_map/ppermute | solution.py:25
  10.3 5.2 %collective-permute-start.2 = (bf16[256,128]{1,0:T(8,128)(2,1)S(1)}, bf16[256,128]{1,0:T(8,128)(2,1)S(1)}, u32[]{:S(2)}, u32[]{:S(2)}) collective-permute-start(bf16[256,128]{1,0:T(8,128)(2,1)S(1)} %get-tuple-element.20), channel_id=1, source_target_pairs={{0,3},{1,2},{2,1},{3,0},{4,7},{5,6},{6,5},{7,4},{8,11},{9,10},{10,... | collective-permute-start | bytes 196616 | tf_op jit(solution)/shard_map/ppermute | solution.py:25
  10.9 7.6 %collective-permute-start.7 = (bf16[216,64]{1,0:T(8,128)(2,1)S(1)}, bf16[216,64]{1,0:T(8,128)(2,1)S(1)}, u32[]{:S(2)}, u32[]{:S(2)}) collective-permute-start(bf16[216,64]{1,0:T(8,128)(2,1)S(1)} %pad_maximum_fusion.refs_4_), channel_id=1, source_target_pairs={{0,3},{1,2},{2,1},{3,0},{4,7},{5,6},{6,5},{7,4},{8,11},{9,10},{10,... | collective-permute-start | bytes 82952 | tf_op jit(solution)/shard_map/ppermute | solution.py:25
  13.4 5.1 %collective-permute-start.6 = (bf16[216,64]{1,0:T(8,128)(2,1)S(1)}, bf16[216,64]{1,0:T(8,128)(2,1)S(1)}, u32[]{:S(2)}, u32[]{:S(2)}) collective-permute-start(bf16[216,64]{1,0:T(8,128)(2,1)S(1)} %pad_maximum_fusion.refs_4_), channel_id=1, source_target_pairs={{0,2},{1,3},{2,0},{3,1},{4,6},{5,7},{6,4},{7,5},{8,10},{9,11},{10,... | collective-permute-start | bytes 82952 | tf_op jit(solution)/shard_map/ppermute | solution.py:25
  13.9 4.6 %collective-permute-start.5 = (bf16[216,64]{1,0:T(8,128)(2,1)S(1)}, bf16[216,64]{1,0:T(8,128)(2,1)S(1)}, u32[]{:S(2)}, u32[]{:S(2)}) collective-permute-start(bf16[216,64]{1,0:T(8,128)(2,1)S(1)} %pad_maximum_fusion.refs_4_), channel_id=1, source_target_pairs={{0,1},{1,0},{2,3},{3,2},{4,5},{5,4},{6,7},{7,6},{8,9},{9,8},{10,11... | collective-permute-start | bytes 82952 | tf_op jit(solution)/shard_map/ppermute | solution.py:25
  18.5 8.7 %copy-start = (bf16[8,216,216]{2,1,0:T(8,128)(2,1)S(1)}, bf16[8,216,216]{2,1,0:T(8,128)(2,1)}, u32[]{:S(2)}) copy-start(bf16[8,216,216]{2,1,0:T(8,128)(2,1)} %refs_4_.3) | copy-start | bytes 2239492
  18.5 8.7 %copy-start.1 = (bf16[216,128]{1,0:T(8,128)(2,1)S(1)}, bf16[216,128]{1,0:T(8,128)(2,1)}, u32[]{:S(2)}) copy-start(bf16[216,128]{1,0:T(8,128)(2,1)} %incoming.1) | copy-start | bytes 165892
  21.5 5.1 %collective-permute-start.8 = (bf16[216,128]{1,0:T(8,128)(2,1)S(1)}, bf16[216,128]{1,0:T(8,128)(2,1)S(1)}, u32[]{:S(2)}, u32[]{:S(2)}) collective-permute-start(bf16[216,128]{1,0:T(8,128)(2,1)S(1)} %get-tuple-element.26), channel_id=1, source_target_pairs={{0,3},{1,2},{2,1},{3,0},{4,7},{5,6},{6,5},{7,4},{8,11},{9,10},{10,... | collective-permute-start | bytes 165896 | tf_op jit(solution)/shard_map/ppermute | solution.py:25
  23.0 4.2 %collective-permute-start.9 = (bf16[216,128]{1,0:T(8,128)(2,1)S(1)}, bf16[216,128]{1,0:T(8,128)(2,1)S(1)}, u32[]{:S(2)}, u32[]{:S(2)}) collective-permute-start(bf16[216,128]{1,0:T(8,128)(2,1)S(1)} %get-tuple-element.27), channel_id=1, source_target_pairs={{0,2},{1,3},{2,0},{3,1},{4,6},{5,7},{6,4},{7,5},{8,10},{9,11},{10,... | collective-permute-start | bytes 165896 | tf_op jit(solution)/shard_map/ppermute | solution.py:25
  23.0 4.2 %collective-permute-start.10 = (bf16[216,128]{1,0:T(8,128)(2,1)S(1)}, bf16[216,128]{1,0:T(8,128)(2,1)S(1)}, u32[]{:S(2)}, u32[]{:S(2)}) collective-permute-start(bf16[216,128]{1,0:T(8,128)(2,1)S(1)} %get-tuple-element.28), channel_id=1, source_target_pairs={{0,1},{1,0},{2,3},{3,2},{4,5},{5,4},{6,7},{7,6},{8,9},{9,8},{10,11... | collective-permute-start | bytes 165896 | tf_op jit(solution)/shard_map/ppermute | solution.py:25
where the time goes:
time: 29 us; the launch traced here: 28.9 us
  starting transfers between devices  15.7 us (54%)
  Pallas kernels  9.7 us (33%)
  waiting for transfers between devices  3.22 us (11%)
    ppermute x9, starting transfers between devices, swap(): return lax.ppermute(x, 'sub', [(i, i ^ r) for i in range(n)])  10.6 us
    ppermute x1, starting transfers between devices, far_field(): lax.ppermute(to_pair, 'slab', [(i, i ^ 1) for i in range(n_slab)])  4.48 us
    ppermute x9, waiting for transfers between devices, swap(): return lax.ppermute(x, 'sub', [(i, i ^ r) for i in range(n)])  3.21 us
    pallas_call x1, Pallas kernels, pick(): pl.pallas_call(functools.partial(pick_kernel, order, n_sub), out_shape=[j...  3 us
    pallas_call x1, Pallas kernels, apply_ops(): pl.pallas_call(functools.partial(apply_kernel, order, n_sub), out_shape=[...  2.95 us
    pallas_call x1, Pallas kernels, up(): pl.pallas_call(functools.partial(up_kernel, n_sub, cells), out_shape=[jax...  2.09 us
    pallas_call x1, Pallas kernels, down(): pl.pallas_call(functools.partial(down_kernel, len(parts)), out_shape=jax....  1.66 us
    ppermute x1, starting transfers between devices, far_field(): lax.ppermute(to_other, 'slab', [(i, (i + 1 ^ 1) - 1) for i in range(1, n_...  0.66 us
  transfers between devices with their start and end apart: 11, of which 3 were waited for; matrix products, arithmetic and copies ran while one was open for 0% of the time, Pallas kernels for 10%

commit v1 on v0

--- a/solution.py
+++ b/solution.py
@@ -167,7 +167,10 @@
         count = each_bit(pack(hits[n], n_ops), add, count)
     for a in range(GROUP):
         todo[count + a] = n_ops * n_tiles
-    return hits, count, lax.div(count + GROUP - 1, GROUP)
+    full = lax.div(count, GROUP)
+    rest = count - full * GROUP
+    short = jnp.logical_and(rest > 0, rest <= GROUP // 2)
+    return hits, jnp.where(rest > GROUP // 2, full + 1, full), short
 
 
 def one_hots(row, base, first_tile, n_tiles):
@@ -190,7 +193,7 @@
     cells = loads[0].shape[1]
     for r in range(n_sub):
         win[r * cells // TILE, :, r * cells % TILE : r * cells % TILE + cells] = loads[r][:order, :]
-    hits, _, trips = list_units(order, loads, n_ops, idx, code0, todo)
+    hits, full, short = list_units(order, loads, n_ops, idx, code0, todo)
 
     used = jnp.where(iota((n_ops, 1), 0) == n_ops - 1, 1.0, functools.reduce(jnp.maximum, hits))
     used = pack(used, n_ops)
@@ -208,9 +211,9 @@
 
     each_bit(used, start, jnp.int32(0))
 
-    def body(i, carry):
+    def gather(i, size):
         base = code0[...]
-        for a in range(GROUP):
+        for a in range(size):
             u = todo[GROUP * i + a]
             k = lax.div(u, n_tiles)
             row = idx[u - k * n_tiles, pl.ds(k, 1), :]
@@ -219,9 +222,17 @@
                 part = jnp.dot(win[t], hot, preferred_element_type=F32)
                 total = part if total is None else total + part
             picked[GROUP * i + a] = total.astype(BF16)
+
+    def body(i, carry):
+        gather(i, GROUP)
         return carry
 
-    lax.fori_loop(0, trips, body, 0)
+    lax.fori_loop(0, full, body, 0)
+
+    @pl.when(short)
+    def _():
+        gather(full, GROUP // 2)
+
     each_bit(used, wait, jnp.int32(0))
 
 
@@ -236,12 +247,12 @@
         at = i // 2 * LANES
         pair = jnp.concatenate([sides[i][...], sides[i + 1][...]], axis=1)
         win[at // TILE, :, at % TILE : at % TILE + LANES] = pair
-    _, _, trips = list_units(order, loads, n_ops, idx, code0, todo)
+    _, full, short = list_units(order, loads, n_ops, idx, code0, todo)
     acc[...] = jnp.zeros_like(acc)
 
-    def gather(i):
+    def gather(i, size):
         base = code0[...]
-        for a in range(GROUP):
+        for a in range(size):
             u = todo[GROUP * i + a]
             k = lax.div(u, n_tiles)
             row = idx[u - k * n_tiles, pl.ds(k, 1), :]
@@ -251,8 +262,8 @@
                 total = part if total is None else total + part
             cols[i & 1, a] = total.astype(BF16) + picked[GROUP * i + a]
 
-    def apply(i):
-        for a in range(GROUP):
+    def apply(i, size):
+        for a in range(size):
             u = todo[GROUP * i + a]
             k = lax.div(u, n_tiles)
             acc[u - k * n_tiles] += jnp.dot(
@@ -260,15 +271,31 @@
             )
 
     def body(i, carry):
-        apply(i - 1)
-        gather(i)
+        apply(i - 1, GROUP)
+        gather(i, GROUP)
         return carry
 
-    @pl.when(trips > 0)
-    def _():
-        gather(0)
-        lax.fori_loop(1, trips, body, 0)
-        apply(trips - 1)
+    @pl.when(full > 0)
+    def _():
+        gather(0, GROUP)
+        lax.fori_loop(1, full, body, 0)
+
+    @pl.when(jnp.logical_and(full > 0, jnp.logical_not(short)))
+    def _():
+        apply(full - 1, GROUP)
+
+    @pl.when(jnp.logical_and(full > 0, short))
+    def _():
+        apply(full - 1, GROUP)
+        gather(full, GROUP // 2)
+
+    @pl.when(jnp.logical_and(full == 0, short))
+    def _():
+        gather(full, GROUP // 2)
+
+    @pl.when(short)
+    def _():
+        apply(full, GROUP // 2)
 
     for j, out in enumerate(outs):
         out[...] = acc[j * cells // TILE, :, j * cells % TILE : j * cells % TILE + cells].astype(out.dtype)

time: 29 us -> 29 us (level)
  no operation moved by 1% of the time
where the time goes in v1:
time: 29 us; the launch traced here: 28.9 us
  starting transfers between devices  15.7 us (54%)
  Pallas kernels  9.72 us (34%)
  waiting for transfers between devices  3.22 us (11%)
    ppermute x9, starting transfers between devices, swap(): return lax.ppermute(x, 'sub', [(i, i ^ r) for i in range(n)])  10.6 us
    ppermute x1, starting transfers between devices, far_field(): lax.ppermute(to_pair, 'slab', [(i, i ^ 1) for i in range(n_slab)])  4.48 us
    ppermute x9, waiting for transfers between devices, swap(): return lax.ppermute(x, 'sub', [(i, i ^ r) for i in range(n)])  3.21 us
    pallas_call x1, Pallas kernels, pick(): pl.pallas_call(functools.partial(pick_kernel, order, n_sub), out_shape=[j...  3 us
    pallas_call x1, Pallas kernels, apply_ops(): pl.pallas_call(functools.partial(apply_kernel, order, n_sub), out_shape=[...  2.97 us
    pallas_call x1, Pallas kernels, up(): pl.pallas_call(functools.partial(up_kernel, n_sub, cells), out_shape=[jax...  2.09 us
    pallas_call x1, Pallas kernels, down(): pl.pallas_call(functools.partial(down_kernel, len(parts)), out_shape=jax....  1.66 us
    ppermute x1, starting transfers between devices, far_field(): lax.ppermute(to_other, 'slab', [(i, (i + 1 ^ 1) - 1) for i in range(1, n_...  0.66 us
  transfers between devices with their start and end apart: 11, of which 3 were waited for; matrix products, arithmetic and copies ran while one was open for 0% of the time, Pallas kernels for 10%

profile of v1, /device:TPU:0, one launch (start us, length us, event | category | flops | bytes accessed | tf_op | source)
XLA Modules:
  0.0 28.9 jit_solution(13746513672221788425)
XLA Ops:
  0.0 2.1 %up.1 = (bf16[256,128]{1,0:T(8,128)(2,1)S(1)}, bf16[256,128]{1,0:T(8,128)(2,1)S(1)}, bf16[256,128]{1,0:T(8,128)(2,1)S(1)}, bf16[256,128]{1,0:T(8,128)(2,1)S(1)},...) custom-call(bf16[216,1024]{1,0:T(8,128)(2,1)} %child_hbm.1, bf16[8,216,216]{2,1,0:T(8,128)(2,1)} %ops_hbm.1, ...), custom_call_target="tpu_custom_call" | custom-call | flops 1073741824 | bytes 2097152 | tf_op jit(solution)/shard_map/up/pallas_call | solution.py:110
  2.1 0.7 %collective-permute-start.3 = (bf16[216,32]{1,0:T(8,128)(2,1)S(1)}, bf16[216,32]{1,0:T(8,128)(2,1)S(1)}, u32[]{:S(2)}, u32[]{:S(2)}) collective-permute-start(bf16[216,32]{1,0:T(8,128)(2,1)S(1)} %get-tuple-element.21), channel_id=1, source_target_pairs={{4,8},{8,4},{12,16},{16,12},{20,24},{24,20},{5,9},{9,5},{13,17},{1... | collective-permute-start | bytes 41480 | tf_op jit(solution)/shard_map/ppermute | solution.py:414
  2.8 4.5 %collective-permute-start.4 = (bf16[216,32]{1,0:T(8,128)(2,1)S(1)}, bf16[216,32]{1,0:T(8,128)(2,1)S(1)}, u32[]{:S(2)}, u32[]{:S(2)}) collective-permute-start(bf16[216,32]{1,0:T(8,128)(2,1)S(1)} %get-tuple-element.22), channel_id=1, source_target_pairs={{0,4},{4,0},{8,12},{12,8},{16,20},{20,16},{24,28},{28,24},{1,5},{5... | collective-permute-start | bytes 41480 | tf_op jit(solution)/shard_map/ppermute | solution.py:413
  7.2 1.5 %collective-permute-start = (bf16[256,128]{1,0:T(8,128)(2,1)S(1)}, bf16[256,128]{1,0:T(8,128)(2,1)S(1)}, u32[]{:S(2)}, u32[]{:S(2)}) collective-permute-start(bf16[256,128]{1,0:T(8,128)(2,1)S(1)} %get-tuple-element.18), channel_id=1, source_target_pairs={{0,1},{1,0},{2,3},{3,2},{4,5},{5,4},{6,7},{7,6},{8,9},{9,8},{10,11... | collective-permute-start | bytes 196616 | tf_op jit(solution)/shard_map/ppermute | solution.py:25
  8.7 1.5 %collective-permute-start.1 = (bf16[256,128]{1,0:T(8,128)(2,1)S(1)}, bf16[256,128]{1,0:T(8,128)(2,1)S(1)}, u32[]{:S(2)}, u32[]{:S(2)}) collective-permute-start(bf16[256,128]{1,0:T(8,128)(2,1)S(1)} %get-tuple-element.19), channel_id=1, source_target_pairs={{0,2},{1,3},{2,0},{3,1},{4,6},{5,7},{6,4},{7,5},{8,10},{9,11},{10,... | collective-permute-start | bytes 196616 | tf_op jit(solution)/shard_map/ppermute | solution.py:25
  10.3 0.5 %collective-permute-start.2 = (bf16[256,128]{1,0:T(8,128)(2,1)S(1)}, bf16[256,128]{1,0:T(8,128)(2,1)S(1)}, u32[]{:S(2)}, u32[]{:S(2)}) collective-permute-start(bf16[256,128]{1,0:T(8,128)(2,1)S(1)} %get-tuple-element.20), channel_id=1, source_target_pairs={{0,3},{1,2},{2,1},{3,0},{4,7},{5,6},{6,5},{7,4},{8,11},{9,10},{10,... | collective-permute-start | bytes 196616 | tf_op jit(solution)/shard_map/ppermute | solution.py:25
  10.7 0.0 collective-permute-done.3
  10.7 0.0 collective-permute-done.4
  10.8 0.1 pad_maximum_fusion.refs_4_
  10.9 2.5 %collective-permute-start.7 = (bf16[216,64]{1,0:T(8,128)(2,1)S(1)}, bf16[216,64]{1,0:T(8,128)(2,1)S(1)}, u32[]{:S(2)}, u32[]{:S(2)}) collective-permute-start(bf16[216,64]{1,0:T(8,128)(2,1)S(1)} %pad_maximum_fusion.refs_4_), channel_id=1, source_target_pairs={{0,3},{1,2},{2,1},{3,0},{4,7},{5,6},{6,5},{7,4},{8,11},{9,10},{10,... | collective-permute-start | bytes 82952 | tf_op jit(solution)/shard_map/ppermute | solution.py:25
  13.4 0.5 %collective-permute-start.6 = (bf16[216,64]{1,0:T(8,128)(2,1)S(1)}, bf16[216,64]{1,0:T(8,128)(2,1)S(1)}, u32[]{:S(2)}, u32[]{:S(2)}) collective-permute-start(bf16[216,64]{1,0:T(8,128)(2,1)S(1)} %pad_maximum_fusion.refs_4_), channel_id=1, source_target_pairs={{0,2},{1,3},{2,0},{3,1},{4,6},{5,7},{6,4},{7,5},{8,10},{9,11},{10,... | collective-permute-start | bytes 82952 | tf_op jit(solution)/shard_map/ppermute | solution.py:25
  13.9 0.0 collective-permute-done.refs_1_
  13.9 0.5 %collective-permute-start.5 = (bf16[216,64]{1,0:T(8,128)(2,1)S(1)}, bf16[216,64]{1,0:T(8,128)(2,1)S(1)}, u32[]{:S(2)}, u32[]{:S(2)}) collective-permute-start(bf16[216,64]{1,0:T(8,128)(2,1)S(1)} %pad_maximum_fusion.refs_4_), channel_id=1, source_target_pairs={{0,1},{1,0},{2,3},{3,2},{4,5},{5,4},{6,7},{7,6},{8,9},{9,8},{10,11... | collective-permute-start | bytes 82952 | tf_op jit(solution)/shard_map/ppermute | solution.py:25
  14.4 0.0 collective-permute-done.1.refs_2_
  14.4 1.0 %collective-permute-done.2.refs_3_ = bf16[256,128]{1,0:T(8,128)(2,1)S(1)} collective-permute-done((bf16[256,128]{1,0:T(8,128)(2,1)S(1)}, bf16[256,128]{1,0:T(8,128)(2,1)S(1)}, u32[]{:S(2)}, u32[]{:S(2)}) %collective-permute-start.2) | collective-permute-done | bytes 65568 | tf_op jit(solution)/shard_map/ppermute | solution.py:25
  15.5 3.0 %pick.1 = (bf16[88,216,256]{2,1,0:T(8,128)(2,1)S(1)}, bf16[40,216,216]{2,1,0:T(8,128)(2,1)S(1)}) custom-call(bf16[256,128]{1,0:T(8,128)(2,1)S(1)} %get-tuple-element.17.refs_0_, bf16[256,128]{1,0:T(8,128)(2,1)S(1)} %collective-permute-done.refs_1_, bf16[256,128]{1,0:T(8,128)(2,1)S(1)} %collective-permute-done.1.refs_2_, ...), custom_call_target="tpu_custom_call" | custom-call | flops 4294967296 | bytes 4194304 | tf_op jit(solution)/shard_map/pick/pallas_call | solution.py:313
  18.5 0.0 collective-permute-done.7.refs_7_
  18.5 0.0 collective-permute-done.6.refs_6_
  18.5 0.0 collective-permute-done.5.refs_5_
  18.5 0.0 copy-start
  18.5 0.0 copy-start.1
  18.5 3.0 %apply.1 = (f32[216,128]{1,0:T(8,128)S(1)}, bf16[216,128]{1,0:T(8,128)(2,1)S(1)}, bf16[216,128]{1,0:T(8,128)(2,1)S(1)}, bf16[216,128]{1,0:T(8,128)(2,1)S(1)}) custom-call(bf16[256,128]{1,0:T(8,128)(2,1)S(1)} %get-tuple-element.17.refs_0_, bf16[256,128]{1,0:T(8,128)(2,1)S(1)} %collective-permute-done.refs_1_, ...), custom_call_target="tpu_custom_call" | custom-call | flops 4294967296 | bytes 4194304 | tf_op jit(solution)/shard_map/apply/pallas_call | solution.py:334
  21.5 1.5 %collective-permute-start.8 = (bf16[216,128]{1,0:T(8,128)(2,1)S(1)}, bf16[216,128]{1,0:T(8,128)(2,1)S(1)}, u32[]{:S(2)}, u32[]{:S(2)}) collective-permute-start(bf16[216,128]{1,0:T(8,128)(2,1)S(1)} %get-tuple-element.26), channel_id=1, source_target_pairs={{0,3},{1,2},{2,1},{3,0},{4,7},{5,6},{6,5},{7,4},{8,11},{9,10},{10,... | collective-permute-start | bytes 165896 | tf_op jit(solution)/shard_map/ppermute | solution.py:25
  23.0 0.0 collective-permute-start.9
  23.0 2.0 %collective-permute-start.10 = (bf16[216,128]{1,0:T(8,128)(2,1)S(1)}, bf16[216,128]{1,0:T(8,128)(2,1)S(1)}, u32[]{:S(2)}, u32[]{:S(2)}) collective-permute-start(bf16[216,128]{1,0:T(8,128)(2,1)S(1)} %get-tuple-element.28), channel_id=1, source_target_pairs={{0,1},{1,0},{2,3},{3,2},{4,5},{5,4},{6,7},{7,6},{8,9},{9,8},{10,11... | collective-permute-start | bytes 165896 | tf_op jit(solution)/shard_map/ppermute | solution.py:25
  25.1 1.6 %collective-permute-done.8.refs_1_ = bf16[216,128]{1,0:T(8,128)(2,1)S(1)} collective-permute-done((bf16[216,128]{1,0:T(8,128)(2,1)S(1)}, bf16[216,128]{1,0:T(8,128)(2,1)S(1)}, u32[]{:S(2)}, u32[]{:S(2)}) %collective-permute-start.8) | collective-permute-done | bytes 55328 | tf_op jit(solution)/shard_map/ppermute | solution.py:25
  26.6 0.6 %collective-permute-done.9.refs_2_ = bf16[216,128]{1,0:T(8,128)(2,1)S(1)} collective-permute-done((bf16[216,128]{1,0:T(8,128)(2,1)S(1)}, bf16[216,128]{1,0:T(8,128)(2,1)S(1)}, u32[]{:S(2)}, u32[]{:S(2)}) %collective-permute-start.9) | collective-permute-done | bytes 55328 | tf_op jit(solution)/shard_map/ppermute | solution.py:25
  27.2 0.0 collective-permute-done.10.refs_3_
  27.2 0.0 copy-done
  27.2 0.0 copy-done.1
  27.2 1.7 %down.1 = f32[216,1024]{1,0:T(8,128)} custom-call(bf16[216,128]{1,0:T(8,128)(2,1)S(1)} %copy-done.1, f32[216,128]{1,0:T(8,128)S(1)} %get-tuple-element.25.refs_0_, bf16[216,128]{1,0:T(8,128)(2,1)S(1)} %collective-permute-done.8.refs_1_, bf16[216,128]{1,0:T(8,128)(2,1)S(1)} %collective-permute-done.9.refs_2_, ...), custom_call_target="tpu_custom_call" | custom-call | flops 1073741824 | bytes 2097152 | tf_op jit(solution)/shard_map/down/pallas_call | solution.py:395
  (1 shorter events, 0.0 us)
Async XLA Ops:
  2.1 8.6 %collective-permute-start.3 = (bf16[216,32]{1,0:T(8,128)(2,1)S(1)}, bf16[216,32]{1,0:T(8,128)(2,1)S(1)}, u32[]{:S(2)}, u32[]{:S(2)}) collective-permute-start(bf16[216,32]{1,0:T(8,128)(2,1)S(1)} %get-tuple-element.21), channel_id=1, source_target_pairs={{4,8},{8,4},{12,16},{16,12},{20,24},{24,20},{5,9},{9,5},{13,17},{1... | collective-permute-start | bytes 41480 | tf_op jit(solution)/shard_map/ppermute | solution.py:414
  2.8 8.0 %collective-permute-start.4 = (bf16[216,32]{1,0:T(8,128)(2,1)S(1)}, bf16[216,32]{1,0:T(8,128)(2,1)S(1)}, u32[]{:S(2)}, u32[]{:S(2)}) collective-permute-start(bf16[216,32]{1,0:T(8,128)(2,1)S(1)} %get-tuple-element.22), channel_id=1, source_target_pairs={{0,4},{4,0},{8,12},{12,8},{16,20},{20,16},{24,28},{28,24},{1,5},{5... | collective-permute-start | bytes 41480 | tf_op jit(solution)/shard_map/ppermute | solution.py:413
  7.2 6.6 %collective-permute-start = (bf16[256,128]{1,0:T(8,128)(2,1)S(1)}, bf16[256,128]{1,0:T(8,128)(2,1)S(1)}, u32[]{:S(2)}, u32[]{:S(2)}) collective-permute-start(bf16[256,128]{1,0:T(8,128)(2,1)S(1)} %get-tuple-element.18), channel_id=1, source_target_pairs={{0,1},{1,0},{2,3},{3,2},{4,5},{5,4},{6,7},{7,6},{8,9},{9,8},{10,11... | collective-permute-start | bytes 196616 | tf_op jit(solution)/shard_map/ppermute | solution.py:25
  8.7 5.7 %collective-permute-start.1 = (bf16[256,128]{1,0:T(8,128)(2,1)S(1)}, bf16[256,128]{1,0:T(8,128)(2,1)S(1)}, u32[]{:S(2)}, u32[]{:S(2)}) collective-permute-start(bf16[256,128]{1,0:T(8,128)(2,1)S(1)} %get-tuple-element.19), channel_id=1, source_target_pairs={{0,2},{1,3},{2,0},{3,1},{4,6},{5,7},{6,4},{7,5},{8,10},{9,11},{10,... | collective-permute-start | bytes 196616 | tf_op jit(solution)/shard_map/ppermute | solution.py:25
  10.3 5.2 %collective-permute-start.2 = (bf16[256,128]{1,0:T(8,128)(2,1)S(1)}, bf16[256,128]{1,0:T(8,128)(2,1)S(1)}, u32[]{:S(2)}, u32[]{:S(2)}) collective-permute-start(bf16[256,128]{1,0:T(8,128)(2,1)S(1)} %get-tuple-element.20), channel_id=1, source_target_pairs={{0,3},{1,2},{2,1},{3,0},{4,7},{5,6},{6,5},{7,4},{8,11},{9,10},{10,... | collective-permute-start | bytes 196616 | tf_op jit(solution)/shard_map/ppermute | solution.py:25
  10.9 7.6 %collective-permute-start.7 = (bf16[216,64]{1,0:T(8,128)(2,1)S(1)}, bf16[216,64]{1,0:T(8,128)(2,1)S(1)}, u32[]{:S(2)}, u32[]{:S(2)}) collective-permute-start(bf16[216,64]{1,0:T(8,128)(2,1)S(1)} %pad_maximum_fusion.refs_4_), channel_id=1, source_target_pairs={{0,3},{1,2},{2,1},{3,0},{4,7},{5,6},{6,5},{7,4},{8,11},{9,10},{10,... | collective-permute-start | bytes 82952 | tf_op jit(solution)/shard_map/ppermute | solution.py:25
  13.4 5.1 %collective-permute-start.6 = (bf16[216,64]{1,0:T(8,128)(2,1)S(1)}, bf16[216,64]{1,0:T(8,128)(2,1)S(1)}, u32[]{:S(2)}, u32[]{:S(2)}) collective-permute-start(bf16[216,64]{1,0:T(8,128)(2,1)S(1)} %pad_maximum_fusion.refs_4_), channel_id=1, source_target_pairs={{0,2},{1,3},{2,0},{3,1},{4,6},{5,7},{6,4},{7,5},{8,10},{9,11},{10,... | collective-permute-start | bytes 82952 | tf_op jit(solution)/shard_map/ppermute | solution.py:25
  13.9 4.6 %collective-permute-start.5 = (bf16[216,64]{1,0:T(8,128)(2,1)S(1)}, bf16[216,64]{1,0:T(8,128)(2,1)S(1)}, u32[]{:S(2)}, u32[]{:S(2)}) collective-permute-start(bf16[216,64]{1,0:T(8,128)(2,1)S(1)} %pad_maximum_fusion.refs_4_), channel_id=1, source_target_pairs={{0,1},{1,0},{2,3},{3,2},{4,5},{5,4},{6,7},{7,6},{8,9},{9,8},{10,11... | collective-permute-start | bytes 82952 | tf_op jit(solution)/shard_map/ppermute | solution.py:25
  18.5 8.7 %copy-start = (bf16[8,216,216]{2,1,0:T(8,128)(2,1)S(1)}, bf16[8,216,216]{2,1,0:T(8,128)(2,1)}, u32[]{:S(2)}) copy-start(bf16[8,216,216]{2,1,0:T(8,128)(2,1)} %refs_4_.3) | copy-start | bytes 2239492
  18.5 8.7 %copy-start.1 = (bf16[216,128]{1,0:T(8,128)(2,1)S(1)}, bf16[216,128]{1,0:T(8,128)(2,1)}, u32[]{:S(2)}) copy-start(bf16[216,128]{1,0:T(8,128)(2,1)} %incoming.1) | copy-start | bytes 165892
  21.5 5.1 %collective-permute-start.8 = (bf16[216,128]{1,0:T(8,128)(2,1)S(1)}, bf16[216,128]{1,0:T(8,128)(2,1)S(1)}, u32[]{:S(2)}, u32[]{:S(2)}) collective-permute-start(bf16[216,128]{1,0:T(8,128)(2,1)S(1)} %get-tuple-element.26), channel_id=1, source_target_pairs={{0,3},{1,2},{2,1},{3,0},{4,7},{5,6},{6,5},{7,4},{8,11},{9,10},{10,... | collective-permute-start | bytes 165896 | tf_op jit(solution)/shard_map/ppermute | solution.py:25
  23.0 4.2 %collective-permute-start.9 = (bf16[216,128]{1,0:T(8,128)(2,1)S(1)}, bf16[216,128]{1,0:T(8,128)(2,1)S(1)}, u32[]{:S(2)}, u32[]{:S(2)}) collective-permute-start(bf16[216,128]{1,0:T(8,128)(2,1)S(1)} %get-tuple-element.27), channel_id=1, source_target_pairs={{0,2},{1,3},{2,0},{3,1},{4,6},{5,7},{6,4},{7,5},{8,10},{9,11},{10,... | collective-permute-start | bytes 165896 | tf_op jit(solution)/shard_map/ppermute | solution.py:25
  23.0 4.2 %collective-permute-start.10 = (bf16[216,128]{1,0:T(8,128)(2,1)S(1)}, bf16[216,128]{1,0:T(8,128)(2,1)S(1)}, u32[]{:S(2)}, u32[]{:S(2)}) collective-permute-start(bf16[216,128]{1,0:T(8,128)(2,1)S(1)} %get-tuple-element.28), channel_id=1, source_target_pairs={{0,1},{1,0},{2,3},{3,2},{4,5},{5,4},{6,7},{7,6},{8,9},{9,8},{10,11... | collective-permute-start | bytes 165896 | tf_op jit(solution)/shard_map/ppermute | solution.py:25
